TPU v7x, 32 devices: a whole 2x2x4 slice. The times are simulated.
32 devices in a mesh: rows: 8 (over z, core), aux: 4 (over y, x).
Axes of the slice: x: 2, y: 2, z: 4, core: 2. Of those that a mesh axis runs over, the one named last changes fastest.
Arguments:
- pair_coeffs: float32 [36000, 8192], P('aux', 'rows'), may hold values from -0.0625 to 0.0625
- pair_gaps: float32 [8192], P('rows'), may hold values from 0.2 to 20
- trial_vectors: float32 [36000, 128], P('aux'), may hold values from -0.03125 to 0.03125
Outputs:
- vectors_out: float32 [36000, 128], P('aux')
- rayleigh: float32 [128, 128], replicated
All inputs are finite; a program needn't handle non-finite values.
Results may differ from a plain program's by a relative error of at most 0.00011.
Values sent between devices are 32-bit elements; how exact they have to be, the bound alone decides.
A program may use at most 128 MiB of HBM per device.

v0:
```python
import functools

import jax
import jax.numpy as jnp
from jax import lax
from jax.experimental import pallas as pl
from jax.experimental.pallas import tpu as pltpu
from jax.sharding import PartitionSpec as P

ITERS = 2
MESH = pl.DeviceIdType.MESH
F32 = jnp.float32
BF16 = jnp.bfloat16
HIGHEST = lax.Precision.HIGHEST


def split(x):
    hi = x.astype(BF16)
    return hi, (x - hi.astype(F32)).astype(BF16)


def reduce_kernel(axis, n, x_ref, o_ref, got, rs_send, rs_recv, ag_send, ag_recv):
    me = lax.axis_index(axis)
    rows = x_ref.shape[0] // n

    def block(i):
        return pl.ds(pl.multiple_of(i * rows, 8), rows)

    barrier = pltpu.get_barrier_semaphore()
    for d in range(1, n):
        pl.semaphore_signal(barrier, inc=1, device_id={axis: lax.rem(me + d, n)}, device_id_type=MESH)
    pl.semaphore_wait(barrier, n - 1)
    scatter = []
    for d in range(1, n):
        to = lax.rem(me + d, n)
        copy = pltpu.make_async_remote_copy(
            x_ref.at[block(to)], got.at[d - 1], rs_send.at[d - 1], rs_recv.at[d - 1],
            device_id={axis: to}, device_id_type=MESH)
        copy.start()
        scatter.append(copy)
    total = x_ref[block(me), :]
    for d in range(1, n):
        scatter[d - 1].wait_recv()
        total = total + got[d - 1]
    o_ref[block(me), :] = total
    gather = []
    for d in range(1, n):
        copy = pltpu.make_async_remote_copy(
            o_ref.at[block(me)], o_ref.at[block(me)], ag_send.at[d - 1], ag_recv.at[d - 1],
            device_id={axis: lax.rem(me + d, n)}, device_id_type=MESH)
        copy.start()
        gather.append(copy)
    for d in range(1, n):
        frm = lax.rem(me + n - d, n)
        pltpu.make_async_remote_copy(
            o_ref.at[block(frm)], o_ref.at[block(frm)], ag_send.at[d - 1], ag_recv.at[d - 1],
            device_id={axis: lax.rem(me + d, n)}, device_id_type=MESH).wait_recv()
    for d in range(1, n):
        scatter[d - 1].wait_send()
        gather[d - 1].wait_send()


def all_reduce(x, axis, n, collective_id):
    if n == 1:
        return x
    rows, cols = x.shape
    return pl.pallas_call(
        functools.partial(reduce_kernel, axis, n),
        out_shape=jax.ShapeDtypeStruct(x.shape, F32),
        in_specs=[pl.BlockSpec(memory_space=pltpu.VMEM)],
        out_specs=pl.BlockSpec(memory_space=pltpu.VMEM),
        scratch_shapes=[pltpu.VMEM((n - 1, rows // n, cols), F32)] + [pltpu.SemaphoreType.DMA((n - 1,))] * 4,
        compiler_params=pltpu.CompilerParams(collective_id=collective_id, has_side_effects=True),
        name="reduce_" + axis,
    )(x)


def apply_kernel(n, rows, b_ref, *refs):
    if rows % 8:
        tail_ref, *refs = refs
    else:
        tail_ref = None
    (s_ref, a_ref, y_ref, c_ref, bbuf, bhi, blo, s2, own, give, pair, came, cat, b_sem,
     pair_send, pair_recv, rs_send, rs_recv, ag_send, ag_recv, fwd_send, fwd_recv) = refs
    h = n // 2
    me = lax.axis_index("rows")
    z, c = me // 2, lax.rem(me, 2)
    at = z + c * (h - 1 - 2 * z)
    step_to = 1 - 2 * c
    steps, blk, k = own.shape
    pairs = s_ref.shape[0]
    last = rows - (steps - 1) * 2 * blk
    last8 = (last + 7) // 8 * 8
    partner = {"rows": z * 2 + 1 - c}
    following = {"rows": (z + step_to) * 2 + c}
    previous = {"rows": (z - step_to) * 2 + c}
    first, end = at == 0, at == h - 1
    delay = 1 + 5 * at
    back = 4 * (h - 1 - at)
    across = 2 * (h - 1)

    def remote(src, dst, send, recv, to):
        return pltpu.make_async_remote_copy(src, dst, send, recv, device_id=to, device_id_type=MESH)

    def over(i):
        return remote(give.at[i], pair.at[i], pair_send.at[i], pair_recv.at[i], partner)

    def onward(i):
        return remote(own.at[i], came.at[i], rs_send.at[i], rs_recv.at[i], following)

    def backward(i):
        return remote(a_ref.at[2 * i + c], a_ref.at[2 * i + c], ag_send.at[i], ag_recv.at[i], previous)

    def share(i, j):
        return remote(a_ref.at[j], a_ref.at[j], fwd_send.at[i], fwd_recv.at[i], partner)

    def full(i):
        return pltpu.make_async_copy(b_ref.at[pl.ds(pl.multiple_of(i * 2 * blk, 2 * blk), 2 * blk)],
                                     bbuf.at[lax.rem(i, 2)], b_sem.at[lax.rem(i, 2)])

    def short():
        src = tail_ref if rows % 8 else b_ref.at[pl.ds((steps - 1) * 2 * blk, last8)]
        slot = (steps - 1) % 2
        return pltpu.make_async_copy(src, bbuf.at[slot, pl.ds(0, last8)], b_sem.at[slot])

    def start(i):
        @pl.when(i < steps - 1)
        def _():
            full(i).start()

        @pl.when(i == steps - 1)
        def _():
            short().start()

    start(jnp.int32(0))
    start(jnp.int32(1))
    hi, lo = split(s_ref[...])
    s2[:, :k] = hi
    s2[:, k:] = lo
    y_ref[...] = jnp.zeros_like(y_ref)
    c_ref[...] = jnp.zeros_like(c_ref)

    barrier = pltpu.get_barrier_semaphore()
    pl.semaphore_signal(barrier, inc=1, device_id=partner, device_id_type=MESH)

    @pl.when(jnp.logical_not(end))
    def _():
        pl.semaphore_signal(barrier, inc=1, device_id=following, device_id_type=MESH)

    @pl.when(jnp.logical_not(first))
    def _():
        pl.semaphore_signal(barrier, inc=1, device_id=previous, device_id_type=MESH)

    pl.semaphore_wait(barrier, 1 + jnp.minimum(at, 1) + jnp.minimum(h - 1 - at, 1))

    def product(i, half):
        where = pl.ds(pl.multiple_of(half * blk, blk), blk)
        keep = pl.ds(pl.multiple_of(i * 2 * blk + half * blk, blk), blk)
        high, low = split(bbuf[lax.rem(i, 2), where, :])
        bhi[keep, :] = high
        blo[keep, :] = low
        wide = jnp.dot(high, s2[...], preferred_element_type=F32)
        thin = jnp.dot(low, s2[:, :k], preferred_element_type=F32)
        return wide[:, :k] + (wide[:, k:] + thin)

    def multiply(i):
        @pl.when(i < steps - 1)
        def _():
            full(i).wait()

        @pl.when(i == steps - 1)
        def _():
            short().wait()
            if last8 < 2 * blk:
                bbuf[(steps - 1) % 2, pl.ds(last8, 2 * blk - last8), :] = jnp.zeros((2 * blk - last8, pairs), F32)

        give[i] = product(i, 1 - c)
        over(i).start()
        own[i] = product(i, c)
        start(i + 2)

    def reduce(i):
        over(i).wait_recv()
        own[i] = own[i] + pair[i]

        @pl.when(jnp.logical_not(first))
        def _():
            onward(i).wait_recv()
            own[i] = own[i] + came[i]

        @pl.when(jnp.logical_not(end))
        def _():
            onward(i).start()

        @pl.when(end)
        def _():
            a_ref[2 * i + c] = own[i]
            backward(i).start()
            share(i, 2 * i + c).start()

    def project(j):
        a = a_ref[j]
        turned = a.T
        c_ref[...] += lax.dot_general(turned, a, (((1,), (0,)), ((), ())), precision=HIGHEST,
                                      preferred_element_type=F32)
        high, low = split(turned)
        cat[:k, :] = high
        cat[k:, :] = low
        keep = pl.ds(pl.multiple_of(j * blk, blk), blk)
        for t in range(pairs // 256):
            cols = pl.ds(t * 256, 256)
            wide = jnp.dot(cat[...], bhi[keep, cols], preferred_element_type=F32)
            thin = jnp.dot(cat[:k, :], blo[keep, cols], preferred_element_type=F32)
            y_ref[:, cols] += wide[:k] + (wide[k:] + thin)

    def body(t, carry):
        @pl.when(t < steps)
        def _():
            multiply(t)

        i = t - delay

        @pl.when(jnp.logical_and(i >= 0, i < steps))
        def _():
            reduce(i)

        i = t - delay - back

        @pl.when(jnp.logical_and(i >= 0, i < steps))
        def _():
            @pl.when(jnp.logical_not(end))
            def _():
                backward(i).wait_recv()
                share(i, 2 * i + c).start()

                @pl.when(jnp.logical_not(first))
                def _():
                    backward(i).start()

            project(2 * i + c)

        i = t - delay - across

        @pl.when(jnp.logical_and(i >= 0, i < steps))
        def _():
            share(i, 2 * i + 1 - c).wait_recv()
            project(2 * i + 1 - c)

        return carry

    total = steps + 1 + 5 * (h - 1) + max(2 * (h - 1), 4 * (h - 1) - 5 * (h - 1))
    lax.fori_loop(0, total, body, 0)

    def drain(i, carry):
        over(i).wait_send()
        share(i, 2 * i + c).wait_send()

        @pl.when(jnp.logical_not(end))
        def _():
            onward(i).wait_send()

        @pl.when(jnp.logical_not(first))
        def _():
            backward(i).wait_send()

        return carry

    lax.fori_loop(0, steps, drain, 0)


def apply(b, s, n):
    rows = b.shape[0]
    pairs, k = s.shape
    blk = 256
    steps = (rows + 2 * blk - 1) // (2 * blk)
    dma = pltpu.SemaphoreType.DMA
    vmem = pl.BlockSpec(memory_space=pltpu.VMEM)
    anywhere = pl.BlockSpec(memory_space=pl.ANY)
    operands = [b]
    if rows % 8:
        operands.append(jnp.pad(b[(steps - 1) * 2 * blk:], ((0, -rows % 8), (0, 0))))
    return pl.pallas_call(
        functools.partial(apply_kernel, n, rows),
        out_shape=(jax.ShapeDtypeStruct((2 * steps, blk, k), F32), jax.ShapeDtypeStruct((k, pairs), F32),
                   jax.ShapeDtypeStruct((k, k), F32)),
        in_specs=[anywhere] * len(operands) + [vmem],
        out_specs=(vmem, vmem, vmem),
        scratch_shapes=[
            pltpu.VMEM((2, 2 * blk, pairs), F32),
            pltpu.VMEM((2 * steps * blk, pairs), BF16),
            pltpu.VMEM((2 * steps * blk, pairs), BF16),
            pltpu.VMEM((pairs, 2 * k), BF16),
            pltpu.VMEM((steps, blk, k), F32),
            pltpu.VMEM((steps, blk, k), F32),
            pltpu.VMEM((steps, blk, k), F32),
            pltpu.VMEM((steps, blk, k), F32),
            pltpu.VMEM((2 * k, blk), BF16),
            dma((2,)),
        ] + [dma((steps,))] * 8,
        compiler_params=pltpu.CompilerParams(collective_id=0, has_side_effects=True,
                                             vmem_limit_bytes=63 * 1024 * 1024),
        name="apply",
    )(*operands, s)


def solution(mesh):
    n = mesh.shape["rows"]
    aux = mesh.shape["aux"]

    def shards(b, gaps, trial):
        rows, k = trial.shape
        weights = (4.0 * gaps / (gaps * gaps + 1.0))[None, :]
        yt = lax.dot_general(trial, b, (((0,), (0,)), ((), ())), precision=lax.Precision.HIGH,
                             preferred_element_type=F32)
        pt = all_reduce(yt, "aux", aux, 1)
        for step in range(ITERS):
            a, yt, gram = apply(b, (pt * weights).T, n)
            both = all_reduce(jnp.concatenate([yt, gram], axis=1), "aux", aux, 2)
            factor = jnp.linalg.cholesky(both[:, -k:])
            inverse = jax.scipy.linalg.solve_triangular(factor, jnp.eye(k, dtype=F32), lower=True)
            pt = jnp.dot(inverse, both[:, :-k], precision=HIGHEST, preferred_element_type=F32)
        v = lax.dot_general(a, inverse, (((2,), (1,)), ((), ())), precision=lax.Precision.HIGH,
                            preferred_element_type=F32)
        vectors = v.reshape(-1, k)[:rows]
        part = lax.dot_general(pt, pt * weights, (((1,), (1,)), ((), ())), precision=HIGHEST,
                               preferred_element_type=F32)
        return vectors, all_reduce(part, "rows", n, 3)

    in_specs = (P("aux", "rows"), P("rows"), P("aux", None))
    return jax.shard_map(shards, mesh=mesh, in_specs=in_specs, out_specs=(P("aux", None), P()), check_vma=False)
```

profile of v0, /device:TPU:0, one launch (start us, length us, event | category | flops | bytes accessed | tf_op | source)
XLA Modules:
  0.0 331.1 jit_solution(11941649634356283565)
XLA Ops:
  0.6 0.7 add_divide_fusion
  1.3 17.7 %fusion.18.x_ref = f32[128,1024]{1,0:T(8,128)} fusion(f32[9000,128]{1,0:T(8,128)} %param.8, f32[9000,1024]{1,0:T(8,128)} %b_ref.3), kind=kOutput, calls=%fused_computation.33 | convolution fusion | flops 7077888000 | bytes 41996288 | tf_op jit(solution)/shard_map/dot_general | solution.py:313
  19.0 20.3 %reduce_aux.3 = f32[128,1024]{1,0:T(8,128)} custom-call(f32[128,1024]{1,0:T(8,128)} %fusion.18.x_ref), custom_call_target="tpu_custom_call" | custom-call | tf_op jit(solution)/shard_map/reduce_aux/pallas_call | solution.py:67
  39.3 1.2 copy.5
  40.5 1.0 multiply_bitcast_fusion.refs_0_
  41.5 86.2 %apply.2 = (f32[36,256,128]{2,1,0:T(8,128)}, f32[128,1024]{1,0:T(8,128)}, f32[128,128]{1,0:T(8,128)}) custom-call(f32[9000,1024]{1,0:T(8,128)} %b_ref.3, f32[1024,128]{1,0:T(8,128)} %multiply_bitcast_fusion.refs_0_), custom_call_target="tpu_custom_call" | custom-call | tf_op jit(solution)/shard_map/apply/pallas_call | solution.py:282
  127.8 1.9 pad_maximum_fusion.x_ref
  129.7 21.6 %reduce_aux.4 = f32[128,1152]{1,0:T(8,128)} custom-call(f32[128,1152]{1,0:T(8,128)} %pad_maximum_fusion.x_ref), custom_call_target="tpu_custom_call" | custom-call | tf_op jit(solution)/shard_map/reduce_aux/pallas_call | solution.py:67
  151.4 0.8 slice.24
  152.3 0.9 fusion.17
  153.2 11.7 %cholesky.44 = f32[128,128]{1,0:T(8,128)S(1)} custom-call(f32[128,128]{1,0:T(8,128)S(1)} %fusion.17), custom_call_target="Cholesky" | custom-call | tf_op jit(solution)/shard_map/jit(cholesky)/cholesky | solution.py:319
  164.9 0.6 compare_reduce_fusion.1
  165.5 0.7 fusion.10
  166.2 9.8 %custom-call.6 = f32[1,128,128]{1,2,0:T(8,128)S(1)} custom-call(f32[1,128,128]{2,1,0:T(8,128)S(1)} %fusion.10), custom_call_target="InvertDiagBlocksLowerTriangular" | custom-call | tf_op jit(solution)/shard_map/jit(_solve_triangular)/triangular_solve | solution.py:320
  176.0 0.3 fusion.8
  176.3 2.9 convolution_multiply_fusion.refs_0_
  179.2 84.0 %apply.3 = (f32[36,256,128]{2,1,0:T(8,128)}, f32[128,1024]{1,0:T(8,128)}, f32[128,128]{1,0:T(8,128)}) custom-call(f32[9000,1024]{1,0:T(8,128)} %b_ref.3, f32[1024,128]{1,0:T(8,128)} %convolution_multiply_fusion.refs_0_), custom_call_target="tpu_custom_call" | custom-call | tf_op jit(solution)/shard_map/apply/pallas_call | solution.py:282
  263.2 1.9 pad_maximum_fusion.1.x_ref
  265.2 20.7 %reduce_aux.5 = f32[128,1152]{1,0:T(8,128)} custom-call(f32[128,1152]{1,0:T(8,128)} %pad_maximum_fusion.1.x_ref), custom_call_target="tpu_custom_call" | custom-call | tf_op jit(solution)/shard_map/reduce_aux/pallas_call | solution.py:67
  285.9 0.8 slice.25
  286.8 0.9 fusion.15
  287.7 11.7 %cholesky.55 = f32[128,128]{1,0:T(8,128)S(1)} custom-call(f32[128,128]{1,0:T(8,128)S(1)} %fusion.15), custom_call_target="Cholesky" | custom-call | tf_op jit(solution)/shard_map/jit(cholesky)/cholesky | solution.py:319
  299.4 0.6 compare_reduce_fusion
  300.1 0.7 fusion.11
  300.7 9.8 %custom-call.7 = f32[1,128,128]{1,2,0:T(8,128)S(1)} custom-call(f32[1,128,128]{2,1,0:T(8,128)S(1)} %fusion.11), custom_call_target="InvertDiagBlocksLowerTriangular" | custom-call | tf_op jit(solution)/shard_map/jit(_solve_triangular)/triangular_solve | solution.py:320
  310.5 0.3 fusion.6
  310.8 1.6 fusion.2
  312.7 1.4 fusion.x_ref
  314.0 10.0 %reduce_rows.1 = f32[128,128]{1,0:T(8,128)} custom-call(f32[128,128]{1,0:T(8,128)} %fusion.x_ref), custom_call_target="tpu_custom_call" | custom-call | tf_op jit(solution)/shard_map/reduce_rows/pallas_call | solution.py:67
  324.1 4.0 %fusion.12 = f32[36,256,128]{2,1,0:T(8,128)S(1)} fusion(f32[36,256,128]{2,1,0:T(8,128)} %get-tuple-element.11, f32[128,128]{1,0:T(8,128)S(1)} %fusion.6), kind=kOutput, calls=%fused_computation.18 | convolution fusion | flops 905969664 | bytes 9502720 | tf_op jit(solution)/shard_map/dot_general | solution.py:322
  328.1 2.3 slice.28
  330.4 0.6 copy.14
  (7 shorter events, 0.4 us)
Async XLA Ops:
  328.1 2.3 copy-start
where the time goes:
time: 332 us; the launch traced here: 331 us
  Pallas kernels  243 us (73%)
  other arithmetic  53 us (16%)
  matrix products  28.2 us (8%)
  local copies, waits for them, and re-layouts  6.24 us (2%)
    pallas_call x2, Pallas kernels, apply(): pl.pallas_call(functools.partial(apply_kernel, n, rows), out_shape=(jax.S...  170 us
    pallas_call x4, Pallas kernels, all_reduce(): pl.pallas_call(functools.partial(reduce_kernel, axis, n), out_shape=jax.S...  72.6 us
    another operation x6, other arithmetic, shards(): factor = jnp.linalg.cholesky(both[:, -k:])  24.8 us
    another operation x4, other arithmetic, shards(): jax.scipy.linalg.solve_triangular(factor, jnp.eye(k, dtype=F32), lower=True)  20.9 us
    dot_general x1, matrix products, shards(): lax.dot_general(trial, b, (((0,), (0,)), ((), ())), precision=lax.Precisi...  17.7 us

commit v1 on v0

v1 whole, which is shorter than its diff:
```python
import functools

import jax
import jax.numpy as jnp
from jax import lax
from jax.experimental import pallas as pl
from jax.experimental.pallas import tpu as pltpu
from jax.sharding import PartitionSpec as P

ITERS = 2
MESH = pl.DeviceIdType.MESH
F32 = jnp.float32
BF16 = jnp.bfloat16
HIGHEST = lax.Precision.HIGHEST


def split(x):
    hi = x.astype(BF16)
    return hi, (x - hi.astype(F32)).astype(BF16)


def kernel(n, m, rows, iters, b_ref, *refs):
    if rows % 8:
        tail_ref, *refs = refs
    else:
        tail_ref = None
    (t_ref, w_ref, v_ref, r_ref, a_ref, bbuf, bhi, blo, s2, own, give, pair, came, cat, y_ref, c_ref,
     whole, got, grams, left, inv, part, gotr,
     b_sem, t_sem, v_sem, pair_send, pair_recv, line_send, line_recv, back_send, back_recv, fwd_send, fwd_recv,
     rs_send, rs_recv, ag_send, ag_recv, g_send, g_recv, r_send, r_recv, q_send, q_recv) = refs
    h = n // 2
    me, mine = lax.axis_index("rows"), lax.axis_index("aux")
    z, c = me // 2, lax.rem(me, 2)
    at = z + c * (h - 1 - 2 * z)
    step_to = 1 - 2 * c
    steps, blk, k = own.shape
    pairs = bhi.shape[1]
    width = pairs // m
    last = rows - (steps - 1) * 2 * blk
    last8 = (last + 7) // 8 * 8
    rows8 = (rows + 7) // 8 * 8
    partner = {"rows": z * 2 + 1 - c}
    following = {"rows": (z + step_to) * 2 + c}
    previous = {"rows": (z - step_to) * 2 + c}
    first, end = at == 0, at == h - 1
    lag = 6
    delay = 1 + 4 * at
    back = 6 * (h - 1 - at) + lag
    across = 3 * (h - 1) + lag

    def remote(src, dst, send, recv, to):
        return pltpu.make_async_remote_copy(src, dst, send, recv, device_id=to, device_id_type=MESH)

    def chunk(j):
        return pl.ds(pl.multiple_of(j * blk, blk), blk)

    def column(i):
        return pl.ds(pl.multiple_of(i * width, 128), width)

    def peer(d):
        return {"aux": lax.rem(mine + d, m)}

    barrier = pltpu.get_barrier_semaphore()
    for d in range(1, n):
        pl.semaphore_signal(barrier, inc=1, device_id={"rows": lax.rem(me + d, n)}, device_id_type=MESH)
    for d in range(1, m):
        pl.semaphore_signal(barrier, inc=1, device_id=peer(d), device_id_type=MESH)

    def full(i):
        return pltpu.make_async_copy(b_ref.at[pl.ds(pl.multiple_of(i * 2 * blk, 2 * blk), 2 * blk)],
                                     bbuf.at[lax.rem(i, 2)], b_sem.at[lax.rem(i, 2)])

    def short():
        src = tail_ref if rows % 8 else b_ref.at[pl.ds((steps - 1) * 2 * blk, last8)]
        slot = (steps - 1) % 2
        return pltpu.make_async_copy(src, bbuf.at[slot, pl.ds(0, last8)], b_sem.at[slot])

    def start(i):
        @pl.when(i < steps - 1)
        def _():
            full(i).start()

        @pl.when(i == steps - 1)
        def _():
            short().start()

    trial = pltpu.make_async_copy(t_ref, a_ref.at[pl.ds(0, rows8)], t_sem.at[0])
    trial.start()
    start(jnp.int32(0))
    start(jnp.int32(1))
    if rows8 < 2 * steps * blk:
        a_ref[pl.ds(rows8, 2 * steps * blk - rows8), :] = jnp.zeros((2 * steps * blk - rows8, k), F32)
    y_ref[...] = jnp.zeros_like(y_ref)
    trial.wait()

    def project(j, with_gram):
        a = a_ref[chunk(j), :]
        turned = a.T
        if with_gram:
            c_ref[...] += lax.dot_general(turned, a, (((1,), (0,)), ((), ())), precision=HIGHEST,
                                          preferred_element_type=F32)
        high, low = split(turned)
        cat[:k, :] = high
        cat[k:, :] = low
        for t in range(pairs // 256):
            cols = pl.ds(t * 256, 256)
            wide = jnp.dot(cat[...], bhi[chunk(j), cols], preferred_element_type=F32)
            thin = jnp.dot(cat[:k, :], blo[chunk(j), cols], preferred_element_type=F32)
            y_ref[:, cols] += wide[:k] + (wide[k:] + thin)

    def load(i, carry):
        @pl.when(i < steps - 1)
        def _():
            full(i).wait()

        @pl.when(i == steps - 1)
        def _():
            short().wait()
            if last8 < 2 * blk:
                bbuf[(steps - 1) % 2, pl.ds(last8, 2 * blk - last8), :] = jnp.zeros((2 * blk - last8, pairs), F32)

        for half in range(2):
            high, low = split(bbuf[lax.rem(i, 2), pl.ds(half * blk, blk), :])
            bhi[chunk(2 * i + half), :] = high
            blo[chunk(2 * i + half), :] = low
        start(i + 2)
        project(2 * i, False)
        project(2 * i + 1, False)
        return carry

    lax.fori_loop(0, steps, load, 0)
    pl.semaphore_wait(barrier, n - 1 + m - 1)

    group = 4

    def eliminate(g, carry):
        j = g * group
        a, x = left[...], inv[...]
        u = [left[pl.ds(j + q, 1), :] for q in range(group)]
        v = [inv[pl.ds(j + q, 1), :] for q in range(group)]
        col = [a[:, q:q + 1] for q in range(group)]
        small = [[u[q][:, p:p + 1] for p in range(group)] for q in range(group)]
        over, low = [], []
        for p in range(group):
            over.append(1.0 / small[p][p])
            for q in range(p + 1, group):
                f = small[q][p] * over[p]
                u[q] = u[q] - f * u[p]
                v[q] = v[q] - f * v[p]
                for r in range(p + 1, group):
                    small[q][r] = small[q][r] - f * small[p][r]
        below = lax.broadcasted_iota(jnp.int32, (k, 1), 0) >= j + group
        for q in range(group):
            top = col[q]
            for p in range(q):
                top = top - low[p] * small[p][q]
            low.append(jnp.where(below, top * over[q], 0.0))
        for q in range(group):
            a = a - low[q] * u[q]
            x = x - low[q] * v[q]
        left[...] = pltpu.roll(a, k - group, 1)
        inv[...] = x
        for q in range(group):
            inv[pl.ds(j + q, 1), :] = v[q] / jnp.sqrt(small[q][q])
        return carry

    def between(e):
        def gram(d, whose):
            return remote(c_ref, grams.at[whose], g_send.at[e, d - 1], g_recv.at[e, d - 1], peer(d))

        def scatter(d):
            return remote(y_ref.at[:, column(lax.rem(mine + d, m))], got.at[d - 1],
                          rs_send.at[e, d - 1], rs_recv.at[e, d - 1], peer(d))

        def gather(d, whose):
            return remote(whole.at[:, column(whose)], whole.at[:, column(whose)],
                          ag_send.at[e, d - 1], ag_recv.at[e, d - 1], peer(d))

        if e:
            for d in range(1, m):
                gram(d, mine).start()
        for d in range(1, m):
            scatter(d).start()

        def sums():
            total = y_ref[:, column(mine)]
            for d in range(1, m):
                scatter(d).wait_recv()
                total = total + got[d - 1]
            whole[:, column(mine)] = total
            for d in range(1, m):
                gather(d, mine).start()

        if e:
            grams[mine] = c_ref[...]
            for d in range(1, m):
                gram(d, lax.rem(mine + m - d, m)).wait_recv()
            total = grams[0]
            for i in range(1, m):
                total = total + grams[i]
            left[...] = total
            inv[...] = (lax.broadcasted_iota(jnp.int32, (k, k), 0)
                        == lax.broadcasted_iota(jnp.int32, (k, k), 1)).astype(F32)
            lax.fori_loop(0, k // group // 2, eliminate, 0)
            sums()
            lax.fori_loop(k // group // 2, k // group, eliminate, 0)
        else:
            sums()
        for d in range(1, m):
            gather(d, lax.rem(mine + m - d, m)).wait_recv()
        if e == iters:
            part[...] = jnp.zeros_like(part)
        for t in range(pairs // 256):
            cols = pl.ds(t * 256, 256)
            pt = whole[:, cols]
            if e:
                pt = jnp.dot(inv[...], pt, precision=HIGHEST, preferred_element_type=F32)
            scaled = pt * w_ref[:, cols]
            if e == iters:
                part[...] += lax.dot_general(pt, scaled, (((1,), (1,)), ((), ())), precision=HIGHEST,
                                             preferred_element_type=F32)
            else:
                high, low = split(scaled.T)
                s2[cols, :k] = high
                s2[cols, k:] = low
        for d in range(1, m):
            if e:
                gram(d, mine).wait_send()
            scatter(d).wait_send()
            gather(d, mine).wait_send()

    def line(e):
        def over(i):
            return remote(give.at[i], pair.at[i], pair_send.at[e, i], pair_recv.at[e, i], partner)

        def onward(i):
            return remote(own.at[i], came.at[i], line_send.at[e, i], line_recv.at[e, i], following)

        def backward(i):
            return remote(a_ref.at[chunk(2 * i + c)], a_ref.at[chunk(2 * i + c)],
                          back_send.at[e, i], back_recv.at[e, i], previous)

        def share(i, j):
            return remote(a_ref.at[chunk(j)], a_ref.at[chunk(j)], fwd_send.at[e, i], fwd_recv.at[e, i], partner)

        def product(j):
            wide = jnp.dot(bhi[chunk(j), :], s2[...], preferred_element_type=F32)
            thin = jnp.dot(blo[chunk(j), :], s2[:, :k], preferred_element_type=F32)
            return wide[:, :k] + (wide[:, k:] + thin)

        def multiply(i):
            give[i] = product(2 * i + 1 - c)
            over(i).start()
            own[i] = product(2 * i + c)

        def reduce(i):
            over(i).wait_recv()
            own[i] = own[i] + pair[i]

            @pl.when(jnp.logical_not(first))
            def _():
                onward(i).wait_recv()
                own[i] = own[i] + came[i]

            @pl.when(jnp.logical_not(end))
            def _():
                onward(i).start()

            @pl.when(end)
            def _():
                a_ref[chunk(2 * i + c), :] = own[i]

        y_ref[...] = jnp.zeros_like(y_ref)
        c_ref[...] = jnp.zeros_like(c_ref)

        def step(t, carry):
            @pl.when(t < steps)
            def _():
                multiply(t)

            i = t - delay

            @pl.when(jnp.logical_and(i >= 0, i < steps))
            def _():
                reduce(i)

            i = t - delay - back

            @pl.when(jnp.logical_and(i >= 0, i < steps))
            def _():
                @pl.when(jnp.logical_not(end))
                def _():
                    backward(i).wait_recv()

                @pl.when(jnp.logical_not(first))
                def _():
                    backward(i).start()

                share(i, 2 * i + c).start()
                project(2 * i + c, True)

            i = t - delay - across

            @pl.when(jnp.logical_and(i >= 0, i < steps))
            def _():
                share(i, 2 * i + 1 - c).wait_recv()
                project(2 * i + 1 - c, True)

            return carry

        lax.fori_loop(0, steps + 1 + 4 * (h - 1) + 6 * (h - 1) + lag, step, 0)

        def drain(i, carry):
            over(i).wait_send()
            share(i, 2 * i + c).wait_send()

            @pl.when(jnp.logical_not(end))
            def _():
                onward(i).wait_send()

            @pl.when(jnp.logical_not(first))
            def _():
                backward(i).wait_send()

            return carry

        lax.fori_loop(0, steps, drain, 0)

    between(0)
    for e in range(iters):
        line(e)
        between(e + 1)

    slab = k // n

    def strip(i):
        return pl.ds(pl.multiple_of(i * slab, 8), slab)

    def scatter(d):
        to = lax.rem(me + d, n)
        return remote(part.at[strip(to)], gotr.at[d - 1], r_send.at[d - 1], r_recv.at[d - 1], {"rows": to})

    def gather(d, whose):
        return remote(r_ref.at[strip(whose)], r_ref.at[strip(whose)], q_send.at[d - 1], q_recv.at[d - 1],
                      {"rows": lax.rem(me + d, n)})

    for d in range(1, n):
        scatter(d).start()

    def rotate(j, carry):
        a_ref[chunk(j), :] = lax.dot_general(a_ref[chunk(j), :], inv[...], (((1,), (1,)), ((), ())),
                                             precision=HIGHEST, preferred_element_type=F32)
        return carry

    lax.fori_loop(0, steps, rotate, 0)
    total = part[strip(me), :]
    for d in range(1, n):
        scatter(d).wait_recv()
        total = total + gotr[d - 1]
    r_ref[strip(me), :] = total
    for d in range(1, n):
        gather(d, me).start()
    lax.fori_loop(steps, 2 * steps, rotate, 0)
    done = pltpu.make_async_copy(a_ref.at[pl.ds(0, rows8)], v_ref, v_sem.at[0])
    done.start()
    for d in range(1, n):
        gather(d, lax.rem(me + n - d, n)).wait_recv()
    for d in range(1, n):
        scatter(d).wait_send()
        gather(d, me).wait_send()
    done.wait()


def solution(mesh):
    n = mesh.shape["rows"]
    m = mesh.shape["aux"]

    def shards(b, gaps, trial):
        rows, k = trial.shape
        pairs = b.shape[1]
        blk = 256
        steps = (rows + 2 * blk - 1) // (2 * blk)
        rows8 = (rows + 7) // 8 * 8
        weights = (4.0 * gaps / (gaps * gaps + 1.0))[None, :]
        dma = pltpu.SemaphoreType.DMA
        vmem = pl.BlockSpec(memory_space=pltpu.VMEM)
        anywhere = pl.BlockSpec(memory_space=pl.ANY)
        operands = [b]
        if rows % 8:
            operands.append(jnp.pad(b[(steps - 1) * 2 * blk:], ((0, -rows % 8), (0, 0))))
            trial = jnp.pad(trial, ((0, -rows % 8), (0, 0)))
        operands.append(trial)
        vectors, rayleigh = pl.pallas_call(
            functools.partial(kernel, n, m, rows, ITERS),
            out_shape=(jax.ShapeDtypeStruct((rows8, k), F32), jax.ShapeDtypeStruct((k, k), F32)),
            in_specs=[anywhere] * len(operands) + [vmem],
            out_specs=(anywhere, vmem),
            scratch_shapes=[
                pltpu.VMEM((2 * steps * blk, k), F32),
                pltpu.VMEM((2, 2 * blk, pairs), F32),
                pltpu.VMEM((2 * steps * blk, pairs), BF16),
                pltpu.VMEM((2 * steps * blk, pairs), BF16),
                pltpu.VMEM((pairs, 2 * k), BF16),
                pltpu.VMEM((steps, blk, k), F32),
                pltpu.VMEM((steps, blk, k), F32),
                pltpu.VMEM((steps, blk, k), F32),
                pltpu.VMEM((steps, blk, k), F32),
                pltpu.VMEM((2 * k, blk), BF16),
                pltpu.VMEM((k, pairs), F32),
                pltpu.VMEM((k, k), F32),
                pltpu.VMEM((k, pairs), F32),
                pltpu.VMEM((m - 1, k, pairs // m), F32),
                pltpu.VMEM((m, k, k), F32),
                pltpu.VMEM((k, k), F32),
                pltpu.VMEM((k, k), F32),
                pltpu.VMEM((k, k), F32),
                pltpu.VMEM((n - 1, k // n, k), F32),
                dma((2,)), dma((1,)), dma((1,)),
            ] + [dma((ITERS, steps))] * 8 + [dma((ITERS + 1, m - 1))] * 6 + [dma((n - 1,))] * 4,
            compiler_params=pltpu.CompilerParams(collective_id=0, has_side_effects=True,
                                                 vmem_limit_bytes=63 * 1024 * 1024),
            name="subspace",
        )(*operands, weights)
        return vectors[:rows], rayleigh

    in_specs = (P("aux", "rows"), P("rows"), P("aux", None))
    return jax.shard_map(shards, mesh=mesh, in_specs=in_specs, out_specs=(P("aux", None), P()), check_vma=False)
```

time: 332 us -> 259 us (0.78)
  other arithmetic: 53 us -> 1.29 us
  matrix products: 28.2 us -> 0 us
  Pallas kernels: 243 us -> 251 us
    another operation x10 -> x0, other arithmetic: 45.7 us -> none  [the longest x6 24.8 us: shards(): factor = jnp.linalg.cholesky(both[:, -k:])]
    dot_general x5 -> x0, matrix products: 27.6 us -> none  [the longest x1 17.7 us: shards(): lax.dot_general(trial, b, (((0,), (0,)), ((), ())), precision=lax.Precisi...]
    pallas_call x6 -> x1, Pallas kernels: 243 us -> 251 us  [shards(): pl.pallas_call(functools.partial(kernel, n, m, rows, ITERS), out_shape=(j...]
    slice x3 -> x0, local copies, waits for them, and re-layouts: 4.01 us -> none  [the longest x1 2.32 us: shards(): vectors = v.reshape(-1, k)[:rows]]
    concatenate x2 -> x0, other arithmetic: 3.88 us -> none  [shards(): both = all_reduce(jnp.concatenate([yt, gram], axis=1), 'aux', aux, 2)]
    unnamed x5 -> x4, local copies, waits for them, and re-layouts: 0.81 us -> 4.62 us
where the time goes in v1:
time: 259 us; the launch traced here: 257 us
  Pallas kernels  251 us (97%)
  local copies, waits for them, and re-layouts  4.62 us (2%)
    pallas_call x1, Pallas kernels, shards(): pl.pallas_call(functools.partial(kernel, n, m, rows, ITERS), out_shape=(j...  251 us

profile of v1, /device:TPU:0, one launch (start us, length us, event | category | flops | bytes accessed | tf_op | source)
XLA Modules:
  0.0 257.1 jit_solution(17248804563093943274)
XLA Ops:
  0.6 1.3 add_divide_fusion
  1.9 250.6 %subspace.1 = (f32[9000,128]{1,0:T(8,128)}, f32[128,128]{1,0:T(8,128)}) custom-call(f32[9000,1024]{1,0:T(8,128)} %b_ref.1, f32[9000,128]{1,0:T(8,128)} %refs_0_.1, f32[1,1024]{1,0:T(1,128)} %bitcast.1), custom_call_target="tpu_custom_call" | custom-call | tf_op jit(solution)/shard_map/subspace/pallas_call | solution.py:393
  252.5 0.0 copy-start
  252.5 4.0 %copy.7 = f32[9000,128]{1,0:T(8,128)} copy(f32[9000,128]{1,0:T(8,128)} %get-tuple-element.4) | data formatting | bytes 9216000
  256.5 0.0 copy-done
  256.5 0.6 copy.8
Async XLA Ops:
  252.5 4.0 %copy-start = (f32[128,128]{1,0:T(8,128)S(1)}, f32[128,128]{1,0:T(8,128)}, u32[]{:S(2)}) copy-start(f32[128,128]{1,0:T(8,128)} %get-tuple-element.5) | copy-start | bytes 196612

commit v2 on v1

--- a/solution.py
+++ b/solution.py
@@ -24,8 +24,8 @@
         tail_ref, *refs = refs
     else:
         tail_ref = None
-    (t_ref, w_ref, v_ref, r_ref, a_ref, bbuf, bhi, blo, s2, own, give, pair, came, cat, y_ref, c_ref,
-     whole, got, grams, left, inv, part, gotr,
+    (t_ref, gap_ref, v_ref, i_ref, r_ref, a_ref, bbuf, bhi, blo, s2, own, give, pair, came, cat, y_ref, c_ref,
+     whole, got, grams, left, inv, part, gotr, w_ref,
      b_sem, t_sem, v_sem, pair_send, pair_recv, line_send, line_recv, back_send, back_recv, fwd_send, fwd_recv,
      rs_send, rs_recv, ag_send, ag_recv, g_send, g_recv, r_send, r_recv, q_send, q_recv) = refs
     h = n // 2
@@ -43,10 +43,10 @@
     following = {"rows": (z + step_to) * 2 + c}
     previous = {"rows": (z - step_to) * 2 + c}
     first, end = at == 0, at == h - 1
-    lag = 6
-    delay = 1 + 4 * at
-    back = 6 * (h - 1 - at) + lag
-    across = 3 * (h - 1) + lag
+    lag, ahead, behind = 6, 4, 6
+    delay = 1 + ahead * at
+    back = behind * (h - 1 - at) + lag
+    across = behind // 2 * (h - 1) + lag
 
     def remote(src, dst, send, recv, to):
         return pltpu.make_async_remote_copy(src, dst, send, recv, device_id=to, device_id_type=MESH)
@@ -91,21 +91,24 @@
     if rows8 < 2 * steps * blk:
         a_ref[pl.ds(rows8, 2 * steps * blk - rows8), :] = jnp.zeros((2 * steps * blk - rows8, k), F32)
     y_ref[...] = jnp.zeros_like(y_ref)
+    gap = gap_ref[...]
+    w_ref[...] = 4.0 * gap / (gap * gap + 1.0)
     trial.wait()
 
-    def project(j, with_gram):
-        a = a_ref[chunk(j), :]
+    def project(at_row, size, with_gram):
+        where = pl.ds(pl.multiple_of(at_row, blk), size)
+        a = a_ref[where, :]
         turned = a.T
         if with_gram:
             c_ref[...] += lax.dot_general(turned, a, (((1,), (0,)), ((), ())), precision=HIGHEST,
                                           preferred_element_type=F32)
         high, low = split(turned)
-        cat[:k, :] = high
-        cat[k:, :] = low
+        cat[:k, :size] = high
+        cat[k:, :size] = low
         for t in range(pairs // 256):
             cols = pl.ds(t * 256, 256)
-            wide = jnp.dot(cat[...], bhi[chunk(j), cols], preferred_element_type=F32)
-            thin = jnp.dot(cat[:k, :], blo[chunk(j), cols], preferred_element_type=F32)
+            wide = jnp.dot(cat[:, :size], bhi[where, cols], preferred_element_type=F32)
+            thin = jnp.dot(cat[:k, :size], blo[where, cols], preferred_element_type=F32)
             y_ref[:, cols] += wide[:k] + (wide[k:] + thin)
 
     def load(i, carry):
@@ -124,45 +127,51 @@
             bhi[chunk(2 * i + half), :] = high
             blo[chunk(2 * i + half), :] = low
         start(i + 2)
-        project(2 * i, False)
-        project(2 * i + 1, False)
+        project(2 * i * blk, 2 * blk, False)
         return carry
 
     lax.fori_loop(0, steps, load, 0)
     pl.semaphore_wait(barrier, n - 1 + m - 1)
 
-    group = 4
-
-    def eliminate(g, carry):
-        j = g * group
-        a, x = left[...], inv[...]
-        u = [left[pl.ds(j + q, 1), :] for q in range(group)]
-        v = [inv[pl.ds(j + q, 1), :] for q in range(group)]
-        col = [a[:, q:q + 1] for q in range(group)]
-        small = [[u[q][:, p:p + 1] for p in range(group)] for q in range(group)]
-        over, low = [], []
-        for p in range(group):
-            over.append(1.0 / small[p][p])
-            for q in range(p + 1, group):
-                f = small[q][p] * over[p]
-                u[q] = u[q] - f * u[p]
-                v[q] = v[q] - f * v[p]
-                for r in range(p + 1, group):
-                    small[q][r] = small[q][r] - f * small[p][r]
-        below = lax.broadcasted_iota(jnp.int32, (k, 1), 0) >= j + group
-        for q in range(group):
-            top = col[q]
-            for p in range(q):
-                top = top - low[p] * small[p][q]
-            low.append(jnp.where(below, top * over[q], 0.0))
-        for q in range(group):
-            a = a - low[q] * u[q]
-            x = x - low[q] * v[q]
-        left[...] = pltpu.roll(a, k - group, 1)
-        inv[...] = x
-        for q in range(group):
-            inv[pl.ds(j + q, 1), :] = v[q] / jnp.sqrt(small[q][q])
-        return carry
+    group = 8
+
+    def eliminate(tiles):
+        def clear(g, carry):
+            j = g * group
+            u = [jnp.broadcast_to(left[pl.ds(j + q, 1), :], (8, k)) for q in range(group)]
+            v = [jnp.broadcast_to(inv[pl.ds(j + q, 1), :], (8, k)) for q in range(group)]
+            small = [[jnp.broadcast_to(u[q][:, p:p + 1], (8, k)) for p in range(group)] for q in range(group)]
+            over = []
+            for p in range(group):
+                over.append(1.0 / small[p][p])
+                for q in range(p + 1, group):
+                    f = small[q][p] * over[p]
+                    u[q] = u[q] - f * u[p]
+                    v[q] = v[q] - f * v[p]
+                    for r in range(p + 1, group):
+                        small[q][r] = small[q][r] - f * small[p][r]
+            kept = [v[q] / jnp.sqrt(small[q][q]) for q in range(group)]
+            for p in reversed(range(group)):
+                for q in range(p + 1, group):
+                    u[p] = u[p] - small[p][q] * u[q]
+                    v[p] = v[p] - small[p][q] * v[q]
+                u[p] = u[p] * over[p]
+                v[p] = v[p] * over[p]
+            for t in tiles:
+                tile = pl.ds(t * 8, 8)
+                a, x = left[tile, :], inv[tile, :]
+                below = lax.broadcasted_iota(jnp.int32, (8, k), 0) + t * 8 >= j + group
+                for q in range(group):
+                    f = jnp.where(below, left[tile, q:q + 1], 0.0)
+                    a = a - f * u[q]
+                    x = x - f * v[q]
+                left[tile, :] = pltpu.roll(a, k - group, 1)
+                inv[tile, :] = x
+            for q in range(group):
+                inv[pl.ds(j + q, 1), :] = kept[q][:1]
+            return carry
+
+        return clear
 
     def between(e):
         def gram(d, whose):
@@ -201,9 +210,9 @@
             left[...] = total
             inv[...] = (lax.broadcasted_iota(jnp.int32, (k, k), 0)
                         == lax.broadcasted_iota(jnp.int32, (k, k), 1)).astype(F32)
-            lax.fori_loop(0, k // group // 2, eliminate, 0)
+            lax.fori_loop(0, k // group // 2, eliminate(range(k // 8)), 0)
             sums()
-            lax.fori_loop(k // group // 2, k // group, eliminate, 0)
+            lax.fori_loop(k // group // 2, k // group, eliminate(range(k // 16, k // 8)), 0)
         else:
             sums()
         for d in range(1, m):
@@ -297,18 +306,18 @@
                     backward(i).start()
 
                 share(i, 2 * i + c).start()
-                project(2 * i + c, True)
+                project((2 * i + c) * blk, blk, True)
 
             i = t - delay - across
 
             @pl.when(jnp.logical_and(i >= 0, i < steps))
             def _():
                 share(i, 2 * i + 1 - c).wait_recv()
-                project(2 * i + 1 - c, True)
+                project((2 * i + 1 - c) * blk, blk, True)
 
             return carry
 
-        lax.fori_loop(0, steps + 1 + 4 * (h - 1) + 6 * (h - 1) + lag, step, 0)
+        lax.fori_loop(0, steps + 1 + (ahead + behind) * (h - 1) + lag, step, 0)
 
         def drain(i, carry):
             over(i).wait_send()
@@ -329,7 +338,11 @@
     between(0)
     for e in range(iters):
         line(e)
+        if e == iters - 1:
+            done = pltpu.make_async_copy(a_ref.at[pl.ds(0, rows8)], v_ref, v_sem.at[0])
+            done.start()
         between(e + 1)
+    i_ref[...] = inv[...]
 
     slab = k // n
 
@@ -347,12 +360,6 @@
     for d in range(1, n):
         scatter(d).start()
 
-    def rotate(j, carry):
-        a_ref[chunk(j), :] = lax.dot_general(a_ref[chunk(j), :], inv[...], (((1,), (1,)), ((), ())),
-                                             precision=HIGHEST, preferred_element_type=F32)
-        return carry
-
-    lax.fori_loop(0, steps, rotate, 0)
     total = part[strip(me), :]
     for d in range(1, n):
         scatter(d).wait_recv()
@@ -360,15 +367,27 @@
     r_ref[strip(me), :] = total
     for d in range(1, n):
         gather(d, me).start()
-    lax.fori_loop(steps, 2 * steps, rotate, 0)
-    done = pltpu.make_async_copy(a_ref.at[pl.ds(0, rows8)], v_ref, v_sem.at[0])
-    done.start()
     for d in range(1, n):
         gather(d, lax.rem(me + n - d, n)).wait_recv()
     for d in range(1, n):
         scatter(d).wait_send()
         gather(d, me).wait_send()
     done.wait()
+
+
+def rotate_kernel(a_ref, i_ref, v_ref):
+    def thirds(x):
+        high, rest = x.astype(BF16), x - x.astype(BF16).astype(F32)
+        return (high,) + split(rest)
+
+    high, mid, low = thirds(a_ref[...])
+    ihigh, imid, ilow = thirds(i_ref[...].T)
+    k = ihigh.shape[1]
+    both = jnp.concatenate([jnp.concatenate([ihigh, imid], axis=1), jnp.concatenate([imid, ihigh], axis=1)], axis=0)
+    wide = jnp.dot(jnp.concatenate([high, mid], axis=1), both, preferred_element_type=F32)
+    thin = jnp.dot(jnp.concatenate([high, low], axis=1), jnp.concatenate([ilow, ihigh], axis=0),
+                   preferred_element_type=F32)
+    v_ref[...] = wide[:, :k] + (wide[:, k:] + thin)
 
 
 def solution(mesh):
@@ -381,7 +400,6 @@
         blk = 256
         steps = (rows + 2 * blk - 1) // (2 * blk)
         rows8 = (rows + 7) // 8 * 8
-        weights = (4.0 * gaps / (gaps * gaps + 1.0))[None, :]
         dma = pltpu.SemaphoreType.DMA
         vmem = pl.BlockSpec(memory_space=pltpu.VMEM)
         anywhere = pl.BlockSpec(memory_space=pl.ANY)
@@ -390,11 +408,11 @@
             operands.append(jnp.pad(b[(steps - 1) * 2 * blk:], ((0, -rows % 8), (0, 0))))
             trial = jnp.pad(trial, ((0, -rows % 8), (0, 0)))
         operands.append(trial)
-        vectors, rayleigh = pl.pallas_call(
+        applied, inverse, rayleigh = pl.pallas_call(
             functools.partial(kernel, n, m, rows, ITERS),
-            out_shape=(jax.ShapeDtypeStruct((rows8, k), F32), jax.ShapeDtypeStruct((k, k), F32)),
+            out_shape=(jax.ShapeDtypeStruct((rows8, k), F32),) + (jax.ShapeDtypeStruct((k, k), F32),) * 2,
             in_specs=[anywhere] * len(operands) + [vmem],
-            out_specs=(anywhere, vmem),
+            out_specs=(anywhere, vmem, vmem),
             scratch_shapes=[
                 pltpu.VMEM((2 * steps * blk, k), F32),
                 pltpu.VMEM((2, 2 * blk, pairs), F32),
@@ -405,7 +423,7 @@
                 pltpu.VMEM((steps, blk, k), F32),
                 pltpu.VMEM((steps, blk, k), F32),
                 pltpu.VMEM((steps, blk, k), F32),
-                pltpu.VMEM((2 * k, blk), BF16),
+                pltpu.VMEM((2 * k, 2 * blk), BF16),
                 pltpu.VMEM((k, pairs), F32),
                 pltpu.VMEM((k, k), F32),
                 pltpu.VMEM((k, pairs), F32),
@@ -415,13 +433,23 @@
                 pltpu.VMEM((k, k), F32),
                 pltpu.VMEM((k, k), F32),
                 pltpu.VMEM((n - 1, k // n, k), F32),
+                pltpu.VMEM((1, pairs), F32),
                 dma((2,)), dma((1,)), dma((1,)),
             ] + [dma((ITERS, steps))] * 8 + [dma((ITERS + 1, m - 1))] * 6 + [dma((n - 1,))] * 4,
             compiler_params=pltpu.CompilerParams(collective_id=0, has_side_effects=True,
                                                  vmem_limit_bytes=63 * 1024 * 1024),
             name="subspace",
-        )(*operands, weights)
-        return vectors[:rows], rayleigh
+        )(*operands, gaps[None, :])
+        tall = steps * blk
+        vectors = pl.pallas_call(
+            rotate_kernel,
+            grid=((rows + tall - 1) // tall,),
+            out_shape=jax.ShapeDtypeStruct((rows, k), F32),
+            in_specs=[pl.BlockSpec((tall, k), lambda i: (i, 0)), pl.BlockSpec((k, k), lambda i: (0, 0))],
+            out_specs=pl.BlockSpec((tall, k), lambda i: (i, 0)),
+            name="rotate",
+        )(applied, inverse)
+        return vectors, rayleigh
 
     in_specs = (P("aux", "rows"), P("rows"), P("aux", None))
     return jax.shard_map(shards, mesh=mesh, in_specs=in_specs, out_specs=(P("aux", None), P()), check_vma=False)

time: 259 us -> 244 us (0.942)
  Pallas kernels: 251 us -> 243 us
  local copies, waits for them, and re-layouts: 4.62 us -> 0.63 us
    pallas_call x1, Pallas kernels: 251 us -> 236 us  [shards(): pl.pallas_call(functools.partial(kernel, n, m, rows, ITERS), out_shape=(j...]
    pallas_call x0 -> x1, Pallas kernels: none -> 6.08 us  [shards(): pl.pallas_call(rotate_kernel, grid=((rows + tall - 1) // tall,), out_shap...]
    unnamed x4 -> x3, local copies, waits for them, and re-layouts: 4.62 us -> 0.63 us
where the time goes in v2:
time: 244 us
  Pallas kernels  243 us (100%)
    pallas_call x1, Pallas kernels, shards(): pl.pallas_call(functools.partial(kernel, n, m, rows, ITERS), out_shape=(j...  236 us
    pallas_call x1, Pallas kernels, shards(): pl.pallas_call(rotate_kernel, grid=((rows + tall - 1) // tall,), out_shap...  6.08 us

profile of v2, /device:TPU:0, one launch (start us, length us, event | category | flops | bytes accessed | tf_op | source)
XLA Modules:
  0.0 243.8 jit_solution(11996025843965047364)
XLA Ops:
  0.6 236.5 %subspace.1 = (f32[9000,128]{1,0:T(8,128)}, f32[128,128]{1,0:T(8,128)}, f32[128,128]{1,0:T(8,128)}) custom-call(f32[9000,1024]{1,0:T(8,128)} %b_ref.1, f32[9000,128]{1,0:T(8,128)} %refs_0_.1, f32[1,1024]{1,0:T(1,128)} %bitcast.1), custom_call_target="tpu_custom_call" | custom-call | tf_op jit(solution)/shard_map/subspace/pallas_call | solution.py:411
  237.1 0.0 copy-start
  237.1 6.1 %rotate.1 = f32[9000,128]{1,0:T(8,128)} custom-call(f32[9000,128]{1,0:T(8,128)} %get-tuple-element.5.a_ref, f32[128,128]{1,0:T(8,128)} %get-tuple-element.6.i_ref), custom_call_target="tpu_custom_call" | custom-call | tf_op jit(solution)/shard_map/rotate/pallas_call | solution.py:444
  243.2 0.0 copy-done
  243.2 0.6 copy.6
Async XLA Ops:
  237.1 6.1 %copy-start = (f32[128,128]{1,0:T(8,128)S(1)}, f32[128,128]{1,0:T(8,128)}, u32[]{:S(2)}) copy-start(f32[128,128]{1,0:T(8,128)} %get-tuple-element.11) | copy-start | bytes 196612

commit v3 on v2

--- a/solution.py
+++ b/solution.py
@@ -197,8 +197,9 @@
                 scatter(d).wait_recv()
                 total = total + got[d - 1]
             whole[:, column(mine)] = total
-            for d in range(1, m):
-                gather(d, mine).start()
+            if e < iters:
+                for d in range(1, m):
+                    gather(d, mine).start()
 
         if e:
             grams[mine] = c_ref[...]
@@ -215,23 +216,25 @@
             lax.fori_loop(k // group // 2, k // group, eliminate(range(k // 16, k // 8)), 0)
         else:
             sums()
+        if e == iters:
+            pt = jnp.dot(inv[...], whole[:, column(mine)], precision=HIGHEST, preferred_element_type=F32)
+            part[...] = lax.dot_general(pt, pt * w_ref[:, column(mine)], (((1,), (1,)), ((), ())),
+                                        precision=HIGHEST, preferred_element_type=F32)
+            for d in range(1, m):
+                gram(d, mine).wait_send()
+                scatter(d).wait_send()
+            return
         for d in range(1, m):
             gather(d, lax.rem(mine + m - d, m)).wait_recv()
-        if e == iters:
-            part[...] = jnp.zeros_like(part)
         for t in range(pairs // 256):
             cols = pl.ds(t * 256, 256)
             pt = whole[:, cols]
             if e:
                 pt = jnp.dot(inv[...], pt, precision=HIGHEST, preferred_element_type=F32)
             scaled = pt * w_ref[:, cols]
-            if e == iters:
-                part[...] += lax.dot_general(pt, scaled, (((1,), (1,)), ((), ())), precision=HIGHEST,
-                                             preferred_element_type=F32)
-            else:
-                high, low = split(scaled.T)
-                s2[cols, :k] = high
-                s2[cols, k:] = low
+            high, low = split(scaled.T)
+            s2[cols, :k] = high
+            s2[cols, k:] = low
         for d in range(1, m):
             if e:
                 gram(d, mine).wait_send()
@@ -364,6 +367,21 @@
     for d in range(1, n):
         scatter(d).wait_recv()
         total = total + gotr[d - 1]
+
+    def spread(d, whose):
+        return remote(pair.at[whose, pl.ds(0, slab)], pair.at[whose, pl.ds(0, slab)],
+                      ag_send.at[iters, d - 1], ag_recv.at[iters, d - 1], peer(d))
+
+    pair[mine, pl.ds(0, slab), :] = total
+    for d in range(1, m):
+        spread(d, mine).start()
+    for d in range(1, m):
+        spread(d, lax.rem(mine + m - d, m)).wait_recv()
+    total = pair[0, pl.ds(0, slab), :]
+    for i in range(1, m):
+        total = total + pair[i, pl.ds(0, slab), :]
+    for d in range(1, m):
+        spread(d, mine).wait_send()
     r_ref[strip(me), :] = total
     for d in range(1, n):
         gather(d, me).start()

time: 244 us -> 241 us (0.988)
  Pallas kernels: 243 us -> 240 us
    pallas_call x1, Pallas kernels: 236 us -> 234 us  [shards(): pl.pallas_call(functools.partial(kernel, n, m, rows, ITERS), out_shape=(j...]
where the time goes in v3:
time: 241 us
  Pallas kernels  240 us (100%)
    pallas_call x1, Pallas kernels, shards(): pl.pallas_call(functools.partial(kernel, n, m, rows, ITERS), out_shape=(j...  234 us
    pallas_call x1, Pallas kernels, shards(): pl.pallas_call(rotate_kernel, grid=((rows + tall - 1) // tall,), out_shap...  6.08 us

profile of v3, /device:TPU:0, one launch (start us, length us, event | category | flops | bytes accessed | tf_op | source)
XLA Modules:
  0.0 241.1 jit_solution(16897092453450072438)
XLA Ops:
  0.6 233.7 %subspace.1 = (f32[9000,128]{1,0:T(8,128)}, f32[128,128]{1,0:T(8,128)}, f32[128,128]{1,0:T(8,128)}) custom-call(f32[9000,1024]{1,0:T(8,128)} %b_ref.1, f32[9000,128]{1,0:T(8,128)} %refs_0_.1, f32[1,1024]{1,0:T(1,128)} %bitcast.1), custom_call_target="tpu_custom_call" | custom-call | tf_op jit(solution)/shard_map/subspace/pallas_call | solution.py:429
  234.3 0.0 copy-start
  234.4 6.1 %rotate.1 = f32[9000,128]{1,0:T(8,128)} custom-call(f32[9000,128]{1,0:T(8,128)} %get-tuple-element.5.a_ref, f32[128,128]{1,0:T(8,128)} %get-tuple-element.6.i_ref), custom_call_target="tpu_custom_call" | custom-call | tf_op jit(solution)/shard_map/rotate/pallas_call | solution.py:462
  240.4 0.0 copy-done
  240.4 0.6 copy.6
Async XLA Ops:
  234.3 6.1 %copy-start = (f32[128,128]{1,0:T(8,128)S(1)}, f32[128,128]{1,0:T(8,128)}, u32[]{:S(2)}) copy-start(f32[128,128]{1,0:T(8,128)} %get-tuple-element.11) | copy-start | bytes 196612
